TPU v7x, 512 devices: a 8x2x16 block of a 8x8x16 slice. The times are simulated.
512 devices in a mesh: grp: 2 (over y), col: 16 (over z), slc: 8 (over x), bat: 2 (over core).
Axes of the slice: x: 8, y: 2, z: 16, core: 2. Of those that a mesh axis runs over, the one named last changes fastest.
The devices are a block of a 8x8x16 slice.
Arguments:
- site_tensors: bfloat16 [16, 288, 2, 64, 128], P(('grp', 'slc'), 'col'), parts along dimension 0, may hold values from -1.2 to 1.2
- left_edge: float32 [16, 64, 128], P(('grp', 'slc')), parts along dimension 0, may hold values from -0.5 to 0.5
- right_edge: float32 [16, 64, 128], P(('grp', 'slc')), parts along dimension 0, may hold values from -0.5 to 0.5
- order: int32 [576], P(('grp', 'col')), parts along dimension 0, may hold values from 0 to 287, each once
- bitstrings: int32 [128, 288], P(('grp', 'bat')), parts along dimension 0, may hold values 0 or 1
Outputs:
- amplitudes: float32 [2, 128], P(None, ('grp', 'bat')), parts along dimension 1
There are 2 independent parts, one for each index of `grp`. A program takes and returns all parts, laid end to end along the dimension named above; each array names one. Nothing has to cross between parts.
Inputs may be any that keep to these rules, and one draw needn't show every extreme that they name: `order`: a permutation of the 288 qubit indices.
All inputs are finite; a program needn't handle non-finite values. No bound on the sum of `bitstrings` on one device may be relied on, other than what follows from the above.
Results may differ from a plain program's by a relative error of at most 0.0003.
Values sent between devices are 32-bit elements; how exact they have to be, the bound alone decides.
No kernel may reach another device: no remote copies, remote signals or barrier semaphores. Data moves between devices by JAX's collectives and lax.ppermute only.
A program may use at most 64 MiB of HBM per device.

v0:
```python
import jax
import jax.numpy as jnp
from jax import lax
from jax.sharding import PartitionSpec as P


def grouped_exchange(array, axis, split_dim, concat_dim, work, item_dim, out_dim):

    def moved(group):
        return lax.all_to_all(group, axis, split_axis=split_dim, concat_axis=concat_dim, tiled=True)

    items = jax.tree.leaves(array)[0].shape[item_dim]
    ends = [items * k // 2 for k in range(2 + 1)] if items % 2 == 0 else [0, items]
    groups = [
        jax.tree.map(lambda a: lax.slice_in_dim(a, low, high, axis=item_dim), array)
        for low, high in zip(ends, ends[1:])
    ]
    arrived = [moved(group) for group in groups]
    made = [work(group) for group in arrived]
    return jax.tree.map(lambda *parts: jnp.concatenate(parts, axis=out_dim), *made)


def one_axis_at_a_time(array, axes):
    for axis in axes:
        array = lax.psum(array, axis)
    return array


def rotate(block):
    middle = block.shape[-1] // 2
    return jnp.concatenate([-block[..., middle:], block[..., :middle]], axis=-1)


def complex_product(first_factor, second_factor):
    stacked = jnp.concatenate([second_factor, rotate(second_factor)], axis=-2)
    return jnp.einsum("bij,bjk->bik", first_factor, stacked, precision=lax.Precision.HIGHEST)


def closing(boundary, edge):
    middle = boundary.shape[-1] // 2
    real_left = boundary[..., :middle]
    imag_left = boundary[..., middle:]
    real_right = edge[..., :middle]
    imag_right = edge[..., middle:]
    real_part = jnp.sum(real_left * real_right - imag_left * imag_right, axis=(1, 2))
    imag_part = jnp.sum(real_left * imag_right + imag_left * real_right, axis=(1, 2))
    return jnp.stack([real_part, imag_part])


def select_site(tensors, site_bits, position):
    matrices = lax.dynamic_index_in_dim(tensors, position, 0, keepdims=False)
    chosen_bits = lax.dynamic_index_in_dim(site_bits, position, 1, keepdims=False)
    return jnp.where(chosen_bits[:, None, None] == 1, matrices[1], matrices[0])


def column_product(tensors, site_bits):
    site_count = tensors.shape[0]
    leading = select_site(tensors, site_bits, 0)
    return lax.fori_loop(
        1,
        site_count,
        lambda position, carried: complex_product(
            carried, select_site(tensors, site_bits, position)
        ),
        leading,
    )


def on_device(site_tensors, left_edge, right_edge, order, bitstrings):
    col_count = lax.axis_size("col")
    col_index = lax.axis_index("col")
    tensors = site_tensors[0].astype(jnp.float32)
    site_bits = jnp.take(bitstrings, order, axis=1)
    batch_rows = site_bits.shape[0]
    bond_size = left_edge.shape[1]
    product = column_product(tensors, site_bits)
    share = (batch_rows + col_count - 1) // col_count
    padded_rows = share * col_count
    grouped = product.reshape(col_count, share, bond_size, 2 * bond_size)

    def chain_all(received):
        items = received.shape[1]
        start = jnp.broadcast_to(left_edge[0], (items, bond_size, 2 * bond_size))
        final_state = lax.fori_loop(
            0,
            received.shape[0],
            lambda position, carried: complex_product(
                carried, lax.dynamic_index_in_dim(received, position, 0, keepdims=False)
            ),
            start,
        )
        return closing(final_state, right_edge[0])

    closed = grouped_exchange(grouped, "col", 0, 0, chain_all, 1, 1)
    placed = lax.dynamic_update_slice(
        jnp.zeros((2, padded_rows), jnp.float32), closed, (jnp.int32(0), col_index * share)
    )
    return one_axis_at_a_time(placed, ("col", "slc"))


def solution(mesh):
    return jax.shard_map(
        on_device,
        mesh=mesh,
        in_specs=(
            P(("grp", "slc"), "col", None, None, None),
            P(("grp", "slc"), None, None),
            P(("grp", "slc"), None, None),
            P(("grp", "col")),
            P(("grp", "bat"), None),
        ),
        out_specs=P(None, ("grp", "bat")),
        check_vma=False,
    )
```

profile of v0, /device:TPU:80, one launch (start us, length us, event | category | flops | bytes accessed | tf_op | source)
XLA Modules:
  0.0 221.1 jit_solution(14152218848554507790)
XLA Ops:
  0.0 0.8 copy.29
  1.4 0.7 compare_and_fusion
  2.1 1.2 bitcast_convert_fusion
  4.2 48.1 %while.41 = (s32[]{:T(128)}, f32[32,64,128]{2,1,0:T(8,128)S(1)}, s32[32,18]{0,1:T(8,128)S(1)}, f32[18,2,64,128]{3,2,1,0:T(8,128)S(1)}, s32[]{:T(128)}, /*index=5*/s32[]{:T(128)}, s32[]{:T(128)}, s32[]{}) while((s32[]{:T(128)}, f32[32,64,128]{2,1,0:T(8,128)S(1)}, s32[32,18]{0,1:T(8,128)S(1)}, f32[18,2,64,128]{3,2,1,0:T(8,128)S(1)}, s32[]{:T(128)}, ...), condition=%wide.region_1.2_spmd, body=%wide.region_0.1_spmd.sunk | while | flops 404095008 | bytes 9634135 | solution.py:59
  4.9 2.1 fusion.31
  7.7 2.1 fusion.31
  10.5 2.1 fusion.31
  13.4 2.1 fusion.31
  16.2 2.1 fusion.31
  19.0 2.1 fusion.31
  21.9 2.1 fusion.31
  24.7 2.1 fusion.31
  27.5 2.1 fusion.31
  30.3 2.1 fusion.31
  33.2 2.1 fusion.31
  36.0 2.1 fusion.31
  38.8 2.1 fusion.31
  41.7 2.1 fusion.31
  44.5 2.1 fusion.31
  47.3 2.1 fusion.31
  50.2 2.1 fusion.31
  52.3 1.1 fusion.22
  53.4 43.7 %all-to-all-start.1 = ((f32[16,1,64,128]{3,2,1,0:T(8,128)}), f32[16,1,64,128]{3,2,1,0:T(8,128)S(1)}, u32[]{:S(2)}, u32[]{:S(2)}) async-start(f32[16,1,64,128]{3,2,1,0:T(8,128)} %get-tuple-element.282), calls=%async_computation.1 | async-start | bytes 1048576 | tf_op jit(solution)/shard_map/all_to_all | solution.py:10
  97.1 28.9 %all-to-all-done.1 = f32[16,1,64,128]{3,2,1,0:T(8,128)S(1)} async-done(((f32[16,1,64,128]{3,2,1,0:T(8,128)}), f32[16,1,64,128]{3,2,1,0:T(8,128)S(1)}, u32[]{:S(2)}, u32[]{:S(2)}) %all-to-all-start.1) | async-done | bytes 524320 | tf_op jit(solution)/shard_map/all_to_all | solution.py:10
  126.0 6.6 %all-to-all-start = ((f32[16,1,64,128]{3,2,1,0:T(8,128)}), f32[16,1,64,128]{3,2,1,0:T(8,128)S(1)}, u32[]{:S(2)}, u32[]{:S(2)}) async-start(f32[16,1,64,128]{3,2,1,0:T(8,128)} %get-tuple-element.283), calls=%async_computation | async-start | bytes 1048576 | tf_op jit(solution)/shard_map/all_to_all | solution.py:10
  132.5 6.0 %while.43 = (s32[]{:T(128)}, f32[1,64,128]{2,1,0:T(8,128)S(1)}, f32[16,1,64,128]{3,2,1,0:T(8,128)S(1)}, s32[]{:T(128)}) while((s32[]{:T(128)}, f32[1,64,128]{2,1,0:T(8,128)S(1)}, f32[16,1,64,128]{3,2,1,0:T(8,128)S(1)}, s32[]{:T(128)}) %tuple.106), condition=%wide.region_7.8_spmd, body=%wide.region_6.7_spmd.sunk | while | flops 12619778 | bytes 327737 | solution.py:84
  138.5 22.9 %all-to-all-done = f32[16,1,64,128]{3,2,1,0:T(8,128)S(1)} async-done(((f32[16,1,64,128]{3,2,1,0:T(8,128)}), f32[16,1,64,128]{3,2,1,0:T(8,128)S(1)}, u32[]{:S(2)}, u32[]{:S(2)}) %all-to-all-start) | async-done | bytes 524320 | tf_op jit(solution)/shard_map/all_to_all | solution.py:10
  161.4 6.0 %while.42 = (s32[]{:T(128)}, f32[1,64,128]{2,1,0:T(8,128)S(1)}, f32[16,1,64,128]{3,2,1,0:T(8,128)S(1)}, s32[]{:T(128)}) while((s32[]{:T(128)}, f32[1,64,128]{2,1,0:T(8,128)S(1)}, f32[16,1,64,128]{3,2,1,0:T(8,128)S(1)}, s32[]{:T(128)}) %tuple.103), condition=%wide.region_3.4_spmd, body=%wide.region_2.3_spmd.sunk | while | flops 12619778 | bytes 327737 | solution.py:84
  167.4 0.8 subtract_reduce_fusion.1
  168.2 2.6 %maximum_maximum_fusion = f32[2,2]{1,0:T(2,128)S(1)} fusion(f32[1,1]{1,0:T(1,128)} %bitcast.27, f32[1,1]{1,0:T(1,128)} %bitcast.26, f32[1,1]{1,0:T(1,128)} %bitcast.25, f32[1,1]{1,0:T(1,128)} %bitcast.24), kind=kLoop, calls=%fused_computation.50 | loop fusion | flops 12 | bytes 32 | tf_op jit(solution)/shard_map/concatenate | solution.py:20
  170.9 31.7 %psum.14 = f32[2,32]{1,0:T(2,128)S(1)} all-reduce(f32[2,32]{1,0:T(2,128)S(1)} %dynamic_update_slice.3), channel_id=1, replica_groups=mesh['grp'=2,'col'=16,'slc'=8,'bat'=2] {'col'}, use_global_device_ids=true, to_apply=%region_10.11 | all-reduce | flops 64 | bytes 512 | tf_op jit(solution)/shard_map/psum | solution.py:25
  202.6 18.5 %psum.15 = f32[2,32]{1,0:T(2,128)} all-reduce(f32[2,32]{1,0:T(2,128)S(1)} %psum.14), channel_id=1, replica_groups=mesh['grp'=2,'col'=16,'slc'=8,'bat'=2] {'slc'}, use_global_device_ids=true, to_apply=%region_11.12 | all-reduce | flops 64 | bytes 512 | tf_op jit(solution)/shard_map/psum | solution.py:25
  (228 shorter events, 22.9 us)
Async XLA Ops:
  0.0 3.3 %copy-start.1 = (s32[32,288]{1,0:T(8,128)S(1)}, s32[32,288]{1,0:T(8,128)}, u32[]{:S(2)}) copy-start(s32[32,288]{1,0:T(8,128)} %param.15) | copy-start | bytes 110596
  53.4 72.6 %all-to-all-start.1 = ((f32[16,1,64,128]{3,2,1,0:T(8,128)}), f32[16,1,64,128]{3,2,1,0:T(8,128)S(1)}, u32[]{:S(2)}, u32[]{:S(2)}) async-start(f32[16,1,64,128]{3,2,1,0:T(8,128)} %get-tuple-element.282), calls=%async_computation.1 | async-start | bytes 1048576 | tf_op jit(solution)/shard_map/all_to_all | solution.py:10
  126.0 35.5 %all-to-all-start = ((f32[16,1,64,128]{3,2,1,0:T(8,128)}), f32[16,1,64,128]{3,2,1,0:T(8,128)S(1)}, u32[]{:S(2)}, u32[]{:S(2)}) async-start(f32[16,1,64,128]{3,2,1,0:T(8,128)} %get-tuple-element.283), calls=%async_computation | async-start | bytes 1048576 | tf_op jit(solution)/shard_map/all_to_all | solution.py:10
  138.5 28.9 %copy-start = (f32[1,64,128]{2,1,0:T(8,128)S(1)}, f32[1,64,128]{2,1,0:T(8,128)}, u32[]{:S(2)}) copy-start(f32[1,64,128]{2,1,0:T(8,128)} %param.13) | copy-start | bytes 98308
where the time goes:
time: 222 us; the launch traced here: 221 us
  waiting for transfers between devices  51.8 us (23%)
  starting transfers between devices  50.3 us (23%)
  blocking collectives  50.2 us (23%)
  matrix products  44.5 us (20%)
  other arithmetic  17.6 us (8%)
  local copies, waits for them, and re-layouts  4.4 us (2%)
  loops' own time  2.29 us (1%)
    all_to_all x2, waiting for transfers between devices, moved(): lax.all_to_all(group, axis, split_axis=split_dim, concat_axis=concat_dim,...  51.8 us
    all_to_all x2, starting transfers between devices, moved(): lax.all_to_all(group, axis, split_axis=split_dim, concat_axis=concat_dim,...  50.3 us
    psum x2, blocking collectives, one_axis_at_a_time(): array = lax.psum(array, axis)  50.2 us
    dot_general x49, matrix products, complex_product(): jnp.einsum('bij,bjk->bik', first_factor, stacked, precision=lax.Precision...  44.5 us
    neg x49, other arithmetic, rotate(): return jnp.concatenate([-block[..., middle:], block[..., :middle]], axis=-1)  8.91 us
  transfers between devices with their start and end apart: 2, of which 2 were waited for; matrix products, arithmetic and copies ran while one was open for 2% of the time, Pallas kernels for 0%

commit v1 on v0

v1 whole, which is shorter than its diff:
```python
import functools

import jax
import jax.numpy as jnp
from jax import lax
from jax.experimental import pallas as pl
from jax.experimental.pallas import tpu as pltpu
from jax.sharding import Mesh, PartitionSpec as P

F32 = jnp.float32
BF16 = jnp.bfloat16
BLOCK = 4
PREFIX = 4
PARAMS = pltpu.CompilerParams(vmem_limit_bytes=16 * 1024 * 1024)


def lane_sign(rows, width):
    lane = lax.broadcasted_iota(jnp.int32, (rows, width), 1)
    return jnp.where(lane < width // 2, -1.0, 1.0).astype(F32)


def rotated(block, sign):
    return pltpu.roll(block, block.shape[1] // 2, 1) * sign


def split(value):
    high = value.astype(BF16)
    low = (value - high.astype(F32)).astype(BF16)
    return high, low


def dot(a, b):
    return jnp.dot(a, b, preferred_element_type=F32)


def pair_product(first, second, sign):
    width = first.shape[1]
    first_high, first_low = split(first)
    second_high, second_low = split(jnp.concatenate([second, rotated(second, sign)], axis=0))
    half = jnp.concatenate([second_high, second_low], axis=1)
    both = dot(
        jnp.concatenate([first_high, first_low], axis=1),
        jnp.concatenate([half, half], axis=0),
    )
    return both[:, :width] + both[:, width:]


def opening_matrix(left, right, sign):
    bond, width = left.shape
    left_high, left_low = split(left)
    right_high, right_low = split(right)
    gram = lax.dot_general(
        jnp.concatenate([right_high, right_high, right_low, right_low], axis=0),
        jnp.concatenate([left_high, left_low, left_high, left_low], axis=0),
        (((0,), (0,)), ((), ())),
        preferred_element_type=F32,
    )
    return gram[:bond] + rotated(gram[bond:], sign)


def column_kernel(base, order_ref, bits_ref, role_ref, tensors_ref, left_ref, right_ref, out_ref, state_ref, table_ref):
    sites, _, bond, width = tensors_ref.shape
    slots = out_ref.shape[0]
    sign = lane_sign(bond, width)
    mask = role_ref[0]
    first = role_ref[1] == 1
    row = lax.broadcasted_iota(jnp.int32, (bond, width), 0)
    lane = lax.broadcasted_iota(jnp.int32, (bond, width), 1)
    unit = jnp.where(row == lane, 1.0, 0.0).astype(F32)
    opening = jnp.where(first, opening_matrix(left_ref[...], right_ref[...], sign), unit)

    def weights(site):
        halves = []
        for value in range(2):
            tensor = tensors_ref[site, value].astype(F32)
            halves.append(jnp.concatenate([tensor, rotated(tensor, sign)], axis=0).astype(BF16))
        half = jnp.concatenate(halves, axis=1)
        return jnp.concatenate([half, half], axis=0)

    def bit(site, slot):
        return bits_ref[(base + slot) ^ mask, order_ref[site]]

    table = opening
    for site in range(PREFIX):
        high, low = split(table)
        both = dot(jnp.concatenate([high, low], axis=1), weights(site))
        table = jnp.concatenate([both[:, :width], both[:, width:]], axis=0)
    high, low = split(table)
    table_ref[:, :width] = high
    table_ref[:, width:] = low
    for slot in range(slots):
        entry = bit(0, slot)
        for site in range(1, PREFIX):
            entry = entry + bit(site, slot) * (1 << site)
        start = pl.multiple_of(entry * bond, bond)
        state_ref[slot * bond:(slot + 1) * bond, :] = table_ref[pl.ds(start, bond), :]

    for site in range(PREFIX, sites):
        matrix = weights(site)
        for start in range(0, slots, BLOCK):
            both = dot(state_ref[start * bond:(start + BLOCK) * bond, :], matrix)
            for slot in range(start, start + BLOCK):
                part = both[(slot - start) * bond:(slot - start + 1) * bond]
                value = jnp.where(bit(site, slot) == 1, part[:, width:], part[:, :width])
                if site == sites - 1:
                    out_ref[slot] = value
                else:
                    high, low = split(value)
                    state_ref[slot * bond:(slot + 1) * bond, :width] = high
                    state_ref[slot * bond:(slot + 1) * bond, width:] = low


def column_products(base, slots, order, bits, role, tensors, left, right):
    sites, _, bond, width = tensors.shape
    scalar = pl.BlockSpec(memory_space=pltpu.SMEM)
    vector = pl.BlockSpec(memory_space=pltpu.VMEM)
    return pl.pallas_call(
        functools.partial(column_kernel, base),
        out_shape=jax.ShapeDtypeStruct((slots, bond, width), F32),
        in_specs=[scalar, scalar, scalar, vector, vector, vector],
        out_specs=vector,
        scratch_shapes=[
            pltpu.VMEM((slots * bond, 2 * width), BF16),
            pltpu.VMEM(((1 << PREFIX) * bond, 2 * width), BF16),
        ],
        cost_estimate=pl.CostEstimate(
            flops=sites * slots * bond * (2 * width) ** 2, bytes_accessed=slots * bond * width * 8, transcendentals=0
        ),
        compiler_params=PARAMS,
        name="column_products",
    )(order, bits, role, tensors, left, right)


def joined(flag, kept, received, sign):
    before = jnp.where(flag, received, kept)
    after = jnp.where(flag, kept, received)
    return pair_product(before, after, sign)


def join_kernel(role_ref, kept_ref, received_ref, *out_refs):
    items, bond, width = kept_ref.shape
    sign = lane_sign(bond, width)
    flag = role_ref[0] == 1
    per = out_refs[0].shape[0]
    for item in range(items):
        out_refs[item // per][item % per] = joined(flag, kept_ref[item], received_ref[item], sign)


def join(flag, kept, received, outs):
    items, bond, width = kept.shape
    out = jax.ShapeDtypeStruct((items // outs, bond, width), F32)
    vector = pl.BlockSpec(memory_space=pltpu.VMEM)
    return pl.pallas_call(
        join_kernel,
        out_shape=(out,) * outs,
        in_specs=[pl.BlockSpec(memory_space=pltpu.SMEM), vector, vector],
        out_specs=(vector,) * outs,
        compiler_params=PARAMS,
        name="join",
    )(flag, kept, received)


def close_kernel(role_ref, parts_ref, out_ref):
    groups, items, bond, width = parts_ref.shape
    sign = lane_sign(bond, width)
    row = lax.broadcasted_iota(jnp.int32, (bond, width), 0)
    lane = lax.broadcasted_iota(jnp.int32, (bond, width), 1)
    slot = lax.broadcasted_iota(jnp.int32, out_ref.shape, 1)
    which = lax.broadcasted_iota(jnp.int32, out_ref.shape, 0)
    total = jnp.zeros(out_ref.shape, F32)
    for item in range(items):
        chain = [parts_ref[group, item] for group in range(groups)]
        while len(chain) > 1:
            chain = [pair_product(chain[k], chain[k + 1], sign) for k in range(0, len(chain), 2)]
        real = jnp.sum(jnp.where(row == lane, chain[0], 0.0), keepdims=True)
        imag = jnp.sum(jnp.where(row + bond == lane, chain[0], 0.0), keepdims=True)
        value = jnp.where(which == 0, real, imag)
        total = jnp.where(slot == (role_ref[0] ^ item), value, total)
    out_ref[...] = total


def close(base, parts, rows):
    return pl.pallas_call(
        close_kernel,
        out_shape=jax.ShapeDtypeStruct((2, rows), F32),
        in_specs=[pl.BlockSpec(memory_space=pltpu.SMEM), pl.BlockSpec(memory_space=pltpu.VMEM)],
        out_specs=pl.BlockSpec(memory_space=pltpu.VMEM),
        compiler_params=PARAMS,
        name="close",
    )(base, parts)


def shift_of(core, cols):
    return (core * 3) % cols


def partner_pairs(cols, cores, distance):
    pairs = []
    for core in range(cores):
        shift = shift_of(core, cols)
        for col in range(cols):
            role = (col - shift) % cols
            other = ((role ^ distance) + shift) % cols
            pairs.append((col * cores + core, other * cores + core))
    return pairs


def solution(mesh):
    shape = dict(mesh.shape)
    inner = 4
    outer = shape["col"] // inner
    cores = shape["bat"]
    cols = shape["col"]
    fine = Mesh(
        mesh.devices.reshape(shape["grp"], outer, inner, shape["slc"], cores),
        ("grp", "far", "near", "slc", "bat"),
    )

    def on_device(site_tensors, left_edge, right_edge, order, bitstrings):
        rows = bitstrings.shape[0]
        core = lax.axis_index("bat")
        far = lax.axis_index("far")
        col = far * inner + lax.axis_index("near")
        role = (col - shift_of(core, cols) + cols) % cols
        bit0, bit1 = role & 1, (role >> 1) & 1
        mask = bit0 * (rows // 2) + bit1 * (rows // 4)
        first = (col == 0).astype(jnp.int32)
        operands = (order, bitstrings, jnp.stack([mask, first]), site_tensors[0], left_edge[0], right_edge[0])
        sent = column_products(rows // 2, rows // 2, *operands)
        kept = column_products(0, rows // 2, *operands)
        received = lax.ppermute(sent, ("far", "near", "bat"), partner_pairs(cols, cores, 1))
        kept, sent = join(bit0[None], kept, received, 2)
        received = lax.ppermute(sent, ("far", "near", "bat"), partner_pairs(cols, cores, 2))
        (quad,) = join(bit1[None], kept, received, 1)
        items, bond, width = quad.shape
        per = items // outer
        parts = lax.all_to_all(
            quad.reshape(outer, per, bond, width), "far", split_axis=0, concat_axis=0, tiled=True
        )
        base = mask ^ (far * per)
        placed = close(base[None], parts, rows)
        everyone = outer * inner * shape["slc"]
        spread = jnp.broadcast_to(placed, (everyone, 2, rows))
        gathered = lax.all_to_all(spread, ("far", "near", "slc"), split_axis=0, concat_axis=0, tiled=True)
        return jnp.sum(gathered, axis=0)

    return jax.shard_map(
        on_device,
        mesh=fine,
        in_specs=(
            P(("grp", "slc"), ("far", "near"), None, None, None),
            P(("grp", "slc"), None, None),
            P(("grp", "slc"), None, None),
            P(("grp", "far", "near")),
            P(("grp", "bat"), None),
        ),
        out_specs=P(None, ("grp", "bat")),
        check_vma=False,
    )
```

time: 222 us -> 125 us (0.56)
  matrix products: 44.5 us -> 0 us
  waiting for transfers between devices: 51.8 us -> 28.4 us
  blocking collectives: 50.2 us -> 30.3 us
  other arithmetic: 17.6 us -> 0.78 us
  Pallas kernels: 0 us -> 11.3 us
  loops' own time: 2.29 us -> 0 us
    psum x2 -> x0, blocking collectives: 50.2 us -> none  [one_axis_at_a_time(): array = lax.psum(array, axis)]
    dot_general x49 -> x0, matrix products: 44.5 us -> none  [complex_product(): jnp.einsum('bij,bjk->bik', first_factor, stacked, precision=lax.Precision...]
    all_to_all x2 -> x1, waiting for transfers between devices: 51.8 us -> 18.5 us  [on_device(): lax.all_to_all(quad.reshape(outer, per, bond, width), 'far', split_axis=0...]
    all_to_all x0 -> x1, blocking collectives: none -> 30.3 us  [on_device(): lax.all_to_all(spread, ('far', 'near', 'slc'), split_axis=0, concat_axis=...]
    ppermute x0 -> x2, starting transfers between devices: none -> 15.6 us  [the longest x1 9.55 us: on_device(): lax.ppermute(sent, ('far', 'near', 'bat'), partner_pairs(cols, cores, 2))]
    all_to_all x2 -> x1, starting transfers between devices: 50.3 us -> 35.5 us  [on_device(): lax.all_to_all(quad.reshape(outer, per, bond, width), 'far', split_axis=0...]
    pallas_call x0 -> x5, Pallas kernels: none -> 11.3 us  [the longest x2 8.82 us: column_products(): pl.pallas_call(functools.partial(column_kernel, base), out_shape=jax.Shap...]
    ppermute x0 -> x2, waiting for transfers between devices: none -> 9.87 us  [the longest x1 7.14 us: on_device(): lax.ppermute(sent, ('far', 'near', 'bat'), partner_pairs(cols, cores, 2))]
  transfers between devices with their start and end apart: 2 -> 3, of which waited for: 2 -> 3; matrix products, arithmetic and copies ran while one was open for 2% -> 0% of each run, Pallas kernels for 0% -> 4%
where the time goes in v1:
time: 125 us
  starting transfers between devices  51.1 us (41%)
  blocking collectives  30.3 us (24%)
  waiting for transfers between devices  28.4 us (23%)
  Pallas kernels  11.3 us (9%)
  local copies, waits for them, and re-layouts  2.58 us (2%)
    all_to_all x1, starting transfers between devices, on_device(): lax.all_to_all(quad.reshape(outer, per, bond, width), 'far', split_axis=0...  35.5 us
    all_to_all x1, blocking collectives, on_device(): lax.all_to_all(spread, ('far', 'near', 'slc'), split_axis=0, concat_axis=...  30.3 us
    all_to_all x1, waiting for transfers between devices, on_device(): lax.all_to_all(quad.reshape(outer, per, bond, width), 'far', split_axis=0...  18.5 us
    ppermute x1, starting transfers between devices, on_device(): lax.ppermute(sent, ('far', 'near', 'bat'), partner_pairs(cols, cores, 2))  9.55 us
    pallas_call x2, Pallas kernels, column_products(): pl.pallas_call(functools.partial(column_kernel, base), out_shape=jax.Shap...  8.82 us
    ppermute x1, waiting for transfers between devices, on_device(): lax.ppermute(sent, ('far', 'near', 'bat'), partner_pairs(cols, cores, 2))  7.14 us
    ppermute x1, starting transfers between devices, on_device(): lax.ppermute(sent, ('far', 'near', 'bat'), partner_pairs(cols, cores, 1))  6.03 us
    ppermute x1, waiting for transfers between devices, on_device(): lax.ppermute(sent, ('far', 'near', 'bat'), partner_pairs(cols, cores, 1))  2.72 us
  transfers between devices with their start and end apart: 3, of which 3 were waited for; matrix products, arithmetic and copies ran while one was open for 0% of the time, Pallas kernels for 4%

profile of v1, /device:TPU:80, one launch (start us, length us, event | category | flops | bytes accessed | tf_op | source)
XLA Modules:
  0.0 124.5 jit_solution(2148875585958294144)
XLA Ops:
  0.0 0.0 copy-start.1
  0.0 0.0 copy-start.2
  0.0 0.1 pad_add_fusion.role_ref
  0.1 0.0 copy-start.4
  0.1 0.7 copy-done.1
  0.8 0.0 copy-done.2
  0.8 0.0 copy-done.4
  0.8 0.0 copy-start
  0.8 1.1 copy-done
  1.9 0.0 copy-start.3
  1.9 0.8 copy-done.3
  2.6 4.4 %column_products.3 = f32[16,64,128]{2,1,0:T(8,128)S(1)} custom-call(s32[18]{0:T(128)S(1)} %copy-done.4, s32[32,288]{1,0:T(8,128)S(1)} %copy-done.1, s32[2]{0:T(128)S(1)} %pad_add_fusion.role_ref, bf16[18,2,64,128]{3,2,1,0:T(8,128)(2,1)S(1)} %bitcast.9, f32[64,128]{1,0:T(8,128)S(1)} %bitcast.11, f32[64,128]{1,0:T(8,128)S(1)} %bitcast.13), custom_call_target="tpu_custom_call" | custom-call | flops 1207959552 | bytes 1048576 | tf_op jit(solution)/shard_map/column_products/pallas_call | solution.py:117
  7.0 6.0 %collective-permute-start = (f32[16,64,128]{2,1,0:T(8,128)S(1)}, f32[16,64,128]{2,1,0:T(8,128)S(1)}, u32[]{:S(2)}, u32[]{:S(2)}) collective-permute-start(f32[16,64,128]{2,1,0:T(8,128)S(1)} %column_products.3), channel_id=1, source_target_pairs={{0,16},{16,0},{32,48},{48,32},{64,80},{80,64},{96,112},{112,96},{1... | collective-permute-start | bytes 1572872 | tf_op jit(solution)/shard_map/ppermute | solution.py:231
  13.1 4.4 %column_products.2.kept_ref = f32[16,64,128]{2,1,0:T(8,128)S(1)} custom-call(s32[18]{0:T(128)S(1)} %copy-done.4, s32[32,288]{1,0:T(8,128)S(1)} %copy-done.1, s32[2]{0:T(128)S(1)} %pad_add_fusion.role_ref, bf16[18,2,64,128]{3,2,1,0:T(8,128)(2,1)S(1)} %bitcast.10, f32[64,128]{1,0:T(8,128)S(1)} %bitcast.12, f32[64,128]{1,0:T(8,128)S(1)} %bitcast.14), custom_call_target="tpu_custom_call" | custom-call | flops 1207959552 | bytes 1048576 | tf_op jit(solution)/shard_map/column_products/pallas_call | solution.py:117
  17.5 2.7 %collective-permute-done.received_ref = f32[16,64,128]{2,1,0:T(8,128)S(1)} collective-permute-done((f32[16,64,128]{2,1,0:T(8,128)S(1)}, f32[16,64,128]{2,1,0:T(8,128)S(1)}, u32[]{:S(2)}, u32[]{:S(2)}) %collective-permute-start) | collective-permute-done | bytes 524320 | tf_op jit(solution)/shard_map/ppermute | solution.py:231
  20.2 0.6 join.2
  20.8 9.6 %collective-permute-start.1 = (f32[8,64,128]{2,1,0:T(8,128)S(1)}, f32[8,64,128]{2,1,0:T(8,128)S(1)}, u32[]{:S(2)}, u32[]{:S(2)}) collective-permute-start(f32[8,64,128]{2,1,0:T(8,128)S(1)} %get-tuple-element.8), channel_id=1, source_target_pairs={{0,32},{16,48},{32,0},{48,16},{64,96},{80,112},{96,64},{112,80},{1... | collective-permute-start | bytes 786440 | tf_op jit(solution)/shard_map/ppermute | solution.py:233
  30.4 7.1 %collective-permute-done.1.received_ref = f32[8,64,128]{2,1,0:T(8,128)S(1)} collective-permute-done((f32[8,64,128]{2,1,0:T(8,128)S(1)}, f32[8,64,128]{2,1,0:T(8,128)S(1)}, u32[]{:S(2)}, u32[]{:S(2)}) %collective-permute-start.1) | collective-permute-done | bytes 262176 | tf_op jit(solution)/shard_map/ppermute | solution.py:233
  37.5 1.1 join.3
  38.6 35.5 %all-to-all-start = ((f32[4,2,64,128]{3,2,1,0:T(8,128)}), f32[4,2,64,128]{3,2,1,0:T(8,128)S(1)}, u32[]{:S(2)}, u32[]{:S(2)}) async-start(f32[4,2,64,128]{3,2,1,0:T(8,128)} %bitcast.8), calls=%async_computation | async-start | bytes 524288 | tf_op jit(solution)/shard_map/all_to_all | solution.py:237
  74.1 18.5 %all-to-all-done.parts_ref = f32[4,2,64,128]{3,2,1,0:T(8,128)S(1)} async-done(((f32[4,2,64,128]{3,2,1,0:T(8,128)}), f32[4,2,64,128]{3,2,1,0:T(8,128)S(1)}, u32[]{:S(2)}, u32[]{:S(2)}) %all-to-all-start) | async-done | bytes 262176 | tf_op jit(solution)/shard_map/all_to_all | solution.py:237
  92.6 0.8 close.1
  93.5 30.3 %all_to_all.10 = f32[128,2,32]{2,1,0:T(2,128)S(1)} all-to-all(f32[128,2,32]{2,1,0:T(2,128)S(1)} %broadcast_in_dim.15), channel_id=1, replica_groups=mesh['grp'=2,'far'=4,'near'=4,'slc'=8,'bat'=2] {'far','near','slc'}, dimensions={0} | all-to-all | bytes 65536 | tf_op jit(solution)/shard_map/all_to_all | solution.py:244
  123.8 0.7 reduce_sum.9
  (1 shorter events, 0.0 us)
Async XLA Ops:
  0.0 0.8 copy-start.1
  0.0 0.8 copy-start.2
  0.1 0.7 copy-start.4
  0.8 1.1 copy-start
  1.9 0.8 copy-start.3
  7.0 13.2 %collective-permute-start = (f32[16,64,128]{2,1,0:T(8,128)S(1)}, f32[16,64,128]{2,1,0:T(8,128)S(1)}, u32[]{:S(2)}, u32[]{:S(2)}) collective-permute-start(f32[16,64,128]{2,1,0:T(8,128)S(1)} %column_products.3), channel_id=1, source_target_pairs={{0,16},{16,0},{32,48},{48,32},{64,80},{80,64},{96,112},{112,96},{1... | collective-permute-start | bytes 1572872 | tf_op jit(solution)/shard_map/ppermute | solution.py:231
  20.8 16.7 %collective-permute-start.1 = (f32[8,64,128]{2,1,0:T(8,128)S(1)}, f32[8,64,128]{2,1,0:T(8,128)S(1)}, u32[]{:S(2)}, u32[]{:S(2)}) collective-permute-start(f32[8,64,128]{2,1,0:T(8,128)S(1)} %get-tuple-element.8), channel_id=1, source_target_pairs={{0,32},{16,48},{32,0},{48,16},{64,96},{80,112},{96,64},{112,80},{1... | collective-permute-start | bytes 786440 | tf_op jit(solution)/shard_map/ppermute | solution.py:233
  38.6 54.0 %all-to-all-start = ((f32[4,2,64,128]{3,2,1,0:T(8,128)}), f32[4,2,64,128]{3,2,1,0:T(8,128)S(1)}, u32[]{:S(2)}, u32[]{:S(2)}) async-start(f32[4,2,64,128]{3,2,1,0:T(8,128)} %bitcast.8), calls=%async_computation | async-start | bytes 524288 | tf_op jit(solution)/shard_map/all_to_all | solution.py:237

commit v2 on v1

--- a/solution.py
+++ b/solution.py
@@ -58,16 +58,31 @@
     return gram[:bond] + rotated(gram[bond:], sign)
 
 
-def column_kernel(base, order_ref, bits_ref, role_ref, tensors_ref, left_ref, right_ref, out_ref, state_ref, table_ref):
+def column_kernel(
+    base, order_ref, role_ref, bits_hbm, tensors_hbm, left_hbm, right_hbm, out_ref,
+    bits_ref, tensors_ref, left_ref, right_ref, state_ref, table_ref, start_ref, word_ref, words_ref, arrived,
+):
     sites, _, bond, width = tensors_ref.shape
     slots = out_ref.shape[0]
+    copies = [
+        pltpu.make_async_copy(source, target, arrived.at[index])
+        for index, (source, target) in enumerate(
+            (
+                (bits_hbm, bits_ref),
+                (tensors_hbm.at[pl.ds(0, PREFIX)], tensors_ref.at[pl.ds(0, PREFIX)]),
+                (tensors_hbm.at[pl.ds(PREFIX, sites - PREFIX)], tensors_ref.at[pl.ds(PREFIX, sites - PREFIX)]),
+            )
+        )
+    ]
+    for copy in copies:
+        copy.start()
     sign = lane_sign(bond, width)
     mask = role_ref[0]
-    first = role_ref[1] == 1
-    row = lax.broadcasted_iota(jnp.int32, (bond, width), 0)
-    lane = lax.broadcasted_iota(jnp.int32, (bond, width), 1)
-    unit = jnp.where(row == lane, 1.0, 0.0).astype(F32)
-    opening = jnp.where(first, opening_matrix(left_ref[...], right_ref[...], sign), unit)
+    qubit = lax.broadcasted_iota(jnp.int32, (8, bits_ref.shape[1]), 1)
+    place = jnp.zeros(qubit.shape, F32)
+    for site in range(sites):
+        place = jnp.where(qubit == order_ref[site], float(1 << site), place)
+    place = place.astype(BF16)
 
     def weights(site):
         halves = []
@@ -77,31 +92,56 @@
         half = jnp.concatenate(halves, axis=1)
         return jnp.concatenate([half, half], axis=0)
 
-    def bit(site, slot):
-        return bits_ref[(base + slot) ^ mask, order_ref[site]]
-
-    table = opening
-    for site in range(PREFIX):
-        high, low = split(table)
-        both = dot(jnp.concatenate([high, low], axis=1), weights(site))
-        table = jnp.concatenate([both[:, :width], both[:, width:]], axis=0)
-    high, low = split(table)
-    table_ref[:, :width] = high
-    table_ref[:, width:] = low
+    copies[0].wait()
+    word = lax.dot_general(
+        place, bits_ref[...].astype(F32).astype(BF16), (((1,), (1,)), ((), ())), preferred_element_type=F32
+    )
+    word_ref[...] = jnp.zeros(word_ref.shape, jnp.int32)
+    word_ref[:, :word.shape[1]] = word.astype(jnp.int32)
+    to_scalars = pltpu.make_async_copy(word_ref, words_ref, arrived.at[len(copies)])
+    to_scalars.start()
+
+    copies[1].wait()
+    for value in range(2):
+        start_ref[value * bond:(value + 1) * bond, :width] = tensors_ref[0, value]
+    start_ref[:, width:] = jnp.zeros((2 * bond, width), BF16)
+
+    @pl.when(role_ref[1] == 1)
+    def _():
+        edges = [
+            pltpu.make_async_copy(left_hbm, left_ref, arrived.at[len(copies) + 1]),
+            pltpu.make_async_copy(right_hbm, right_ref, arrived.at[len(copies) + 2]),
+        ]
+        for edge in edges:
+            edge.start()
+        for edge in edges:
+            edge.wait()
+        high, low = split(opening_matrix(left_ref[...], right_ref[...], sign))
+        both = dot(jnp.concatenate([high, low], axis=1), weights(0))
+        high, low = split(jnp.concatenate([both[:, :width], both[:, width:]], axis=0))
+        start_ref[:, :width] = high
+        start_ref[:, width:] = low
+
+    operand = start_ref[...]
+    for site in range(1, PREFIX):
+        both = dot(operand, weights(site))
+        high, low = split(jnp.concatenate([both[:, :width], both[:, width:]], axis=0))
+        operand = jnp.concatenate([high, low], axis=1)
+    table_ref[...] = operand
+    to_scalars.wait()
+    words = [words_ref[0, (base + slot) ^ mask] for slot in range(slots)]
     for slot in range(slots):
-        entry = bit(0, slot)
-        for site in range(1, PREFIX):
-            entry = entry + bit(site, slot) * (1 << site)
-        start = pl.multiple_of(entry * bond, bond)
+        start = pl.multiple_of((words[slot] & ((1 << PREFIX) - 1)) * bond, bond)
         state_ref[slot * bond:(slot + 1) * bond, :] = table_ref[pl.ds(start, bond), :]
 
+    copies[2].wait()
     for site in range(PREFIX, sites):
         matrix = weights(site)
         for start in range(0, slots, BLOCK):
             both = dot(state_ref[start * bond:(start + BLOCK) * bond, :], matrix)
             for slot in range(start, start + BLOCK):
                 part = both[(slot - start) * bond:(slot - start + 1) * bond]
-                value = jnp.where(bit(site, slot) == 1, part[:, width:], part[:, :width])
+                value = jnp.where((words[slot] & (1 << site)) != 0, part[:, width:], part[:, :width])
                 if site == sites - 1:
                     out_ref[slot] = value
                 else:
@@ -113,22 +153,30 @@
 def column_products(base, slots, order, bits, role, tensors, left, right):
     sites, _, bond, width = tensors.shape
     scalar = pl.BlockSpec(memory_space=pltpu.SMEM)
-    vector = pl.BlockSpec(memory_space=pltpu.VMEM)
+    far = pl.BlockSpec(memory_space=pltpu.HBM)
     return pl.pallas_call(
         functools.partial(column_kernel, base),
         out_shape=jax.ShapeDtypeStruct((slots, bond, width), F32),
-        in_specs=[scalar, scalar, scalar, vector, vector, vector],
-        out_specs=vector,
+        in_specs=[scalar, scalar, far, far, far, far],
+        out_specs=pl.BlockSpec(memory_space=pltpu.VMEM),
         scratch_shapes=[
+            pltpu.VMEM(bits.shape, jnp.int32),
+            pltpu.VMEM(tensors.shape, BF16),
+            pltpu.VMEM((bond, width), F32),
+            pltpu.VMEM((bond, width), F32),
             pltpu.VMEM((slots * bond, 2 * width), BF16),
             pltpu.VMEM(((1 << PREFIX) * bond, 2 * width), BF16),
+            pltpu.VMEM((2 * bond, 2 * width), BF16),
+            pltpu.VMEM((8, width), jnp.int32),
+            pltpu.SMEM((8, width), jnp.int32),
+            pltpu.SemaphoreType.DMA((6,)),
         ],
         cost_estimate=pl.CostEstimate(
             flops=sites * slots * bond * (2 * width) ** 2, bytes_accessed=slots * bond * width * 8, transcendentals=0
         ),
         compiler_params=PARAMS,
         name="column_products",
-    )(order, bits, role, tensors, left, right)
+    )(order, role, *(pltpu.with_memory_space_constraint(a, pltpu.HBM) for a in (bits, tensors, left, right)))
 
 
 def joined(flag, kept, received, sign):

time: 125 us -> 123 us (0.984)
  Pallas kernels: 11.3 us -> 13.9 us
  local copies, waits for them, and re-layouts: 2.58 us -> 0.69 us
  waiting for transfers between devices: 28.4 us -> 27.1 us
    pallas_call x2, Pallas kernels: 8.82 us -> 11.4 us  [column_products(): pl.pallas_call(functools.partial(column_kernel, base), out_shape=jax.Shap...]
    unnamed x10 -> x2, local copies, waits for them, and re-layouts: 2.55 us -> 0.65 us
    ppermute x1, waiting for transfers between devices: 2.72 us -> 1.44 us  [on_device(): lax.ppermute(sent, ('far', 'near', 'bat'), partner_pairs(cols, cores, 1))]
  transfers between devices with their start and end apart: 3 -> 3, of which waited for: 3 -> 3; matrix products, arithmetic and copies ran while one was open for 0% -> 0% of each run, Pallas kernels for 4% -> 5%
where the time goes in v2:
time: 123 us
  starting transfers between devices  49.9 us (41%)
  blocking collectives  30.3 us (25%)
  waiting for transfers between devices  27.1 us (22%)
  Pallas kernels  13.9 us (11%)
    all_to_all x1, starting transfers between devices, on_device(): lax.all_to_all(quad.reshape(outer, per, bond, width), 'far', split_axis=0...  35.5 us
    all_to_all x1, blocking collectives, on_device(): lax.all_to_all(spread, ('far', 'near', 'slc'), split_axis=0, concat_axis=...  30.3 us
    all_to_all x1, waiting for transfers between devices, on_device(): lax.all_to_all(quad.reshape(outer, per, bond, width), 'far', split_axis=0...  18.5 us
    pallas_call x2, Pallas kernels, column_products(): pl.pallas_call(functools.partial(column_kernel, base), out_shape=jax.Shap...  11.4 us
    ppermute x1, starting transfers between devices, on_device(): lax.ppermute(sent, ('far', 'near', 'bat'), partner_pairs(cols, cores, 2))  9.55 us
    ppermute x1, waiting for transfers between devices, on_device(): lax.ppermute(sent, ('far', 'near', 'bat'), partner_pairs(cols, cores, 2))  7.14 us
    ppermute x1, starting transfers between devices, on_device(): lax.ppermute(sent, ('far', 'near', 'bat'), partner_pairs(cols, cores, 1))  4.82 us
  transfers between devices with their start and end apart: 3, of which 3 were waited for; matrix products, arithmetic and copies ran while one was open for 0% of the time, Pallas kernels for 5%

profile of v2, /device:TPU:80, one launch (start us, length us, event | category | flops | bytes accessed | tf_op | source)
XLA Modules:
  0.0 122.7 jit_solution(9134859154931579859)
XLA Ops:
  0.0 0.1 pad_add_fusion.role_ref
  0.1 0.0 copy-start
  0.1 0.7 copy-done
  0.7 5.7 %column_products.3 = f32[16,64,128]{2,1,0:T(8,128)S(1)} custom-call(s32[18]{0:T(128)S(1)} %copy-done, s32[2]{0:T(128)S(1)} %pad_add_fusion.role_ref, s32[32,288]{1,0:T(8,128)} %bits_hbm.3, bf16[18,2,64,128]{3,2,1,0:T(8,128)(2,1)} %bitcast.9, f32[64,128]{1,0:T(8,128)} %bitcast.11, f32[64,128]{1,0:T(8,128)} %bitcast.13), custom_call_target="tpu_custom_call" | custom-call | flops 1207959552 | bytes 1048576 | tf_op jit(solution)/shard_map/column_products/pallas_call | solution.py:157
  6.4 4.8 %collective-permute-start = (f32[16,64,128]{2,1,0:T(8,128)S(1)}, f32[16,64,128]{2,1,0:T(8,128)S(1)}, u32[]{:S(2)}, u32[]{:S(2)}) collective-permute-start(f32[16,64,128]{2,1,0:T(8,128)S(1)} %column_products.3), channel_id=1, source_target_pairs={{0,16},{16,0},{32,48},{48,32},{64,80},{80,64},{96,112},{112,96},{1... | collective-permute-start | bytes 1572872 | tf_op jit(solution)/shard_map/ppermute | solution.py:279
  11.3 5.7 %column_products.2.kept_ref = f32[16,64,128]{2,1,0:T(8,128)S(1)} custom-call(s32[18]{0:T(128)S(1)} %copy-done, s32[2]{0:T(128)S(1)} %pad_add_fusion.role_ref, s32[32,288]{1,0:T(8,128)} %bits_hbm.3, bf16[18,2,64,128]{3,2,1,0:T(8,128)(2,1)} %bitcast.10, f32[64,128]{1,0:T(8,128)} %bitcast.12, f32[64,128]{1,0:T(8,128)} %bitcast.14), custom_call_target="tpu_custom_call" | custom-call | flops 1207959552 | bytes 1048576 | tf_op jit(solution)/shard_map/column_products/pallas_call | solution.py:157
  17.0 1.4 %collective-permute-done.received_ref = f32[16,64,128]{2,1,0:T(8,128)S(1)} collective-permute-done((f32[16,64,128]{2,1,0:T(8,128)S(1)}, f32[16,64,128]{2,1,0:T(8,128)S(1)}, u32[]{:S(2)}, u32[]{:S(2)}) %collective-permute-start) | collective-permute-done | bytes 524320 | tf_op jit(solution)/shard_map/ppermute | solution.py:279
  18.4 0.6 join.2
  19.0 9.6 %collective-permute-start.1 = (f32[8,64,128]{2,1,0:T(8,128)S(1)}, f32[8,64,128]{2,1,0:T(8,128)S(1)}, u32[]{:S(2)}, u32[]{:S(2)}) collective-permute-start(f32[8,64,128]{2,1,0:T(8,128)S(1)} %get-tuple-element.8), channel_id=1, source_target_pairs={{0,32},{16,48},{32,0},{48,16},{64,96},{80,112},{96,64},{112,80},{1... | collective-permute-start | bytes 786440 | tf_op jit(solution)/shard_map/ppermute | solution.py:281
  28.5 7.1 %collective-permute-done.1.received_ref = f32[8,64,128]{2,1,0:T(8,128)S(1)} collective-permute-done((f32[8,64,128]{2,1,0:T(8,128)S(1)}, f32[8,64,128]{2,1,0:T(8,128)S(1)}, u32[]{:S(2)}, u32[]{:S(2)}) %collective-permute-start.1) | collective-permute-done | bytes 262176 | tf_op jit(solution)/shard_map/ppermute | solution.py:281
  35.7 1.1 join.3
  36.8 35.5 %all-to-all-start = ((f32[4,2,64,128]{3,2,1,0:T(8,128)}), f32[4,2,64,128]{3,2,1,0:T(8,128)S(1)}, u32[]{:S(2)}, u32[]{:S(2)}) async-start(f32[4,2,64,128]{3,2,1,0:T(8,128)} %bitcast.8), calls=%async_computation | async-start | bytes 524288 | tf_op jit(solution)/shard_map/all_to_all | solution.py:285
  72.3 18.5 %all-to-all-done.parts_ref = f32[4,2,64,128]{3,2,1,0:T(8,128)S(1)} async-done(((f32[4,2,64,128]{3,2,1,0:T(8,128)}), f32[4,2,64,128]{3,2,1,0:T(8,128)S(1)}, u32[]{:S(2)}, u32[]{:S(2)}) %all-to-all-start) | async-done | bytes 262176 | tf_op jit(solution)/shard_map/all_to_all | solution.py:285
  90.8 0.8 close.1
  91.7 30.3 %all_to_all.10 = f32[128,2,32]{2,1,0:T(2,128)S(1)} all-to-all(f32[128,2,32]{2,1,0:T(2,128)S(1)} %broadcast_in_dim.15), channel_id=1, replica_groups=mesh['grp'=2,'far'=4,'near'=4,'slc'=8,'bat'=2] {'far','near','slc'}, dimensions={0} | all-to-all | bytes 65536 | tf_op jit(solution)/shard_map/all_to_all | solution.py:292
  122.0 0.7 reduce_sum.9
  (1 shorter events, 0.0 us)
Async XLA Ops:
  0.1 0.7 copy-start
  6.4 12.0 %collective-permute-start = (f32[16,64,128]{2,1,0:T(8,128)S(1)}, f32[16,64,128]{2,1,0:T(8,128)S(1)}, u32[]{:S(2)}, u32[]{:S(2)}) collective-permute-start(f32[16,64,128]{2,1,0:T(8,128)S(1)} %column_products.3), channel_id=1, source_target_pairs={{0,16},{16,0},{32,48},{48,32},{64,80},{80,64},{96,112},{112,96},{1... | collective-permute-start | bytes 1572872 | tf_op jit(solution)/shard_map/ppermute | solution.py:279
  19.0 16.7 %collective-permute-start.1 = (f32[8,64,128]{2,1,0:T(8,128)S(1)}, f32[8,64,128]{2,1,0:T(8,128)S(1)}, u32[]{:S(2)}, u32[]{:S(2)}) collective-permute-start(f32[8,64,128]{2,1,0:T(8,128)S(1)} %get-tuple-element.8), channel_id=1, source_target_pairs={{0,32},{16,48},{32,0},{48,16},{64,96},{80,112},{96,64},{112,80},{1... | collective-permute-start | bytes 786440 | tf_op jit(solution)/shard_map/ppermute | solution.py:281
  36.8 54.0 %all-to-all-start = ((f32[4,2,64,128]{3,2,1,0:T(8,128)}), f32[4,2,64,128]{3,2,1,0:T(8,128)S(1)}, u32[]{:S(2)}, u32[]{:S(2)}) async-start(f32[4,2,64,128]{3,2,1,0:T(8,128)} %bitcast.8), calls=%async_computation | async-start | bytes 524288 | tf_op jit(solution)/shard_map/all_to_all | solution.py:285
